TPU v7x, 256 devices: a 4x2x16 block of a 4x16x16 slice. The times are simulated.
256 devices in a mesh: groups: 2 (over y), patch: 16 (over z), sub: 8 (over x, core).
Axes of the slice: x: 4, y: 2, z: 16, core: 2. Of those that a mesh axis runs over, the one named last changes fastest.
The devices are a block of a 4x16x16 slice.
Arguments:
- fine_nodes: float32 [262144, 128], P(('groups', 'patch', 'sub')), parts along dimension 0, may hold values from -6 to 6
- fine_edges: float32 [262144, 6, 128], P(('groups', 'patch', 'sub')), parts along dimension 0, may hold values from -6 to 6
- fine_senders: int32 [262144, 6], P(('groups', 'patch', 'sub')), parts along dimension 0, may hold values from 0 to 1279
- fine_halo: int32 [512, 128], P(('groups', 'patch', 'sub')), parts along dimension 0, may hold values from 0 to 1023
- fine_pool: int32 [262144], P(('groups', 'patch', 'sub')), parts along dimension 0, may hold values from 0 to 2047, as said below
- quarter_edges: float32 [65536, 4, 128], P(('groups', 'patch')), parts along dimension 0, may hold values from -6 to 6
- quarter_senders: int32 [65536, 4], P(('groups', 'patch')), parts along dimension 0, may hold values from 0 to 2303
- quarter_halo: int32 [64, 128], P(('groups', 'patch')), parts along dimension 0, may hold values from 0 to 2047
- quarter_pool: int32 [65536], P(('groups', 'patch')), parts along dimension 0, may hold values from 0 to 511, as said below
- coarse_edges: float32 [16384, 4, 128], P(('groups', 'patch', 'sub')), parts along dimension 0, may hold values from -6 to 6
- coarse_senders: int32 [16384, 4], P('groups'), parts along dimension 0, may hold values from 0 to 8191
- edge_in: float32 [3, 384, 128], replicated, may hold values from -0.3125 to 0.3125
- edge_out: float32 [3, 128, 128], replicated, may hold values from -0.5 to 0.5
- node_in: float32 [3, 256, 128], replicated, may hold values from -0.375 to 0.375
- node_out: float32 [3, 128, 128], replicated, may hold values from -0.5 to 0.5
Outputs:
- fine_out: float32 [262144, 128], P(('groups', 'patch', 'sub')), parts along dimension 0
There are 2 independent parts, one for each index of `groups`. A program takes and returns all parts, laid end to end along the dimension named above; an argument that names none is the same for every part. Nothing has to cross between parts.
Inputs may be any that keep to these rules, and one draw needn't show every extreme that they name: `fine_pool`: every one of a patch's 2048 quarter nodes is the target of at least one fine node of that patch. `quarter_pool`: every one of a patch's 512 sixteenth nodes is the target of at least one quarter node of that patch.
All inputs are finite; a program needn't handle non-finite values.
Results may differ from a plain program's by a relative error of at most 0.00005.
Values sent between devices are 32-bit elements; how exact they have to be, the bound alone decides.
A program may use at most 128 MiB of HBM per device.

v0:
```python
import functools

import jax
import jax.numpy as jnp
from jax import lax
from jax.experimental import pallas as pl
from jax.experimental.pallas import tpu as pltpu
from jax.sharding import PartitionSpec as P

MESH = pl.DeviceIdType.MESH
BF = jnp.bfloat16
F32 = jnp.float32
W = 128
VMEM_LIMIT = 56 * 1024 * 1024


def split2(x):
    hi = x.astype(BF)
    lo = (x - hi.astype(F32)).astype(BF)
    return jnp.concatenate([hi, lo], axis=1)


def packed(w):
    s = split2(w)
    return jnp.concatenate([s, s], axis=0)


def halves(y):
    return y[:, :W] + y[:, W:]


def dot(a, b):
    return jnp.dot(a, b, preferred_element_type=F32)


def mm(x, wp):
    return halves(dot(split2(x), wp))


def centred_columns(w):
    return w - jnp.mean(w, axis=1, keepdims=True)


def scaled(m):
    return m * lax.rsqrt(jnp.mean(m * m, axis=1, keepdims=True) + 1e-05)


def column(row):
    return jnp.broadcast_to(row, (W, W)).T


def lanes(rows):
    return lax.broadcasted_iota(jnp.int32, (rows, W), 1)


def sublanes(rows):
    return lax.broadcasted_iota(jnp.int32, (rows, W), 0)


def ones_where(mask):
    return jnp.where(mask, 1.0, 0.0).astype(BF)


def one_hot(col, width):
    lane = lanes(col.shape[0])
    return jnp.concatenate([ones_where(col == lane + j * W) for j in range(width // W)], axis=1)


def one_hot_t(index_ref, first, rows, blocks):
    sub = sublanes(rows) + first
    return jnp.concatenate(
        [ones_where(jnp.broadcast_to(index_ref[j : j + 1, :], (rows, W)) == sub) for j in range(blocks)],
        axis=1,
    )


def counts_of(index_ref, first, rows, blocks):
    sub = sublanes(rows) + first

    def add(j, acc):
        row = jnp.broadcast_to(index_ref[pl.ds(j, 1), :], (rows, W))
        return acc + jnp.where(row == sub, 1.0, 0.0)

    acc = lax.fori_loop(0, blocks, add, jnp.zeros((rows, W), F32))
    return jnp.sum(acc, axis=1, keepdims=True)


TILE = 256


class Sends:
    def __init__(self):
        self.all = []

    def __call__(self, src, dst, ss, rs, to):
        c = pltpu.make_async_remote_copy(src, dst, ss, rs, device_id=to, device_id_type=MESH)
        c.start()
        self.all.append(c)
        return c


def node_update(h, summed, node_w, last_w):
    both = jnp.concatenate([split2(h), split2(summed)], axis=1)
    a = jnp.maximum(halves(dot(both, node_w)), 0.0)
    return h + scaled(mm(a, last_w))


def levels_kernel(n_patch, n_sub,
                  nodes, f_edges, f_senders, f_halo, pool, q_edges, q_senders, q_halo, q_pool, c_edges, c_senders,
                  edge_in, edge_out, node_in, node_out,
                  out,
                  nodes_v, fe_v, fs_v, qe_v, qs_v, ce_v, cs_v, ei_v, eo_v, ni_v, no_v,
                  pools, fh_sent, fh_got, table, news, zs, new_v,
                  sums_v, pair_buf, comb, stage, relay_in, arrive,
                  tab, hsent, qall, oh_q, oh_h, oh_c, oh_p, oh_t, base_v,
                  p16, pair16, comb16, stage16, relay16, arrive16, zt, gpart, gstage, grelay, garrive, ctab,
                  load_sem, edge_sem, fh_s, fh_r, pl_s, pl_r,
                  pair_s, pair_r, rs_s, rs_r, ag_s, ag_r, h_s, h_r,
                  pair16_s, pair16_r, rs16_s, rs16_r, qg_s, qg_r, z_s, z_r, d_s, d_r, g_s, g_r, cg_s, cg_r):
    p, me = lax.axis_index("patch"), lax.axis_index("sub")
    core = lax.rem(me, 2)
    x = me // 2
    n_x = n_sub // 2
    partner = {"sub": me + 1 - 2 * core}
    rows = nodes.shape[0]
    degree = f_edges.shape[0]
    tiles = rows // TILE
    q_rows = tab.shape[0] - 2 * W
    share = q_rows // n_sub
    s_rows = p16.shape[0]
    s_share = s_rows // n_sub
    k_q = qs_v.shape[0]
    k_s = cs_v.shape[0]
    send = Sends()

    def column_of(r):
        return lax.rem(x + r, n_x)

    def chip(r):
        return {"sub": 2 * lax.rem(x + r + n_x, n_x) + core}

    def patch(r):
        return {"patch": lax.rem(p + r + n_patch, n_patch)}

    def at(t, size):
        return pl.ds(pl.multiple_of(t * size, size), size)

    def load(src, dst, sem):
        c = pltpu.make_async_copy(src, dst, sem)
        c.start()
        return c

    load_nodes = load(nodes, nodes_v, load_sem.at[0])
    load_ei = load(edge_in, ei_v, load_sem.at[1])
    load_fs = load(f_senders, fs_v, load_sem.at[2])
    for i in range(tiles):
        load(f_edges.at[:, pl.ds(i * TILE, TILE), :], fe_v.at[i], edge_sem.at[i])
    load_rest = [
        load(edge_out, eo_v, load_sem.at[3]),
        load(node_in, ni_v, load_sem.at[4]),
        load(node_out, no_v, load_sem.at[5]),
    ]
    load_later = [
        load(q_edges.at[at(me, share * k_q), :], qe_v, load_sem.at[6]),
        load(q_senders, qs_v, load_sem.at[7]),
        load(c_edges, ce_v, load_sem.at[8]),
        load(c_senders.at[:, at(p, s_rows)], cs_v, load_sem.at[9]),
    ]

    after = {"patch": lax.rem(p + (me + 1) // n_sub, n_patch), "sub": lax.rem(me + 1, n_sub)}
    wrap = (n_sub - me) // n_sub
    before = {"patch": lax.rem(p + n_patch - wrap, n_patch), "sub": lax.rem(me + n_sub - 1, n_sub)}
    peers = [{"sub": lax.rem(me + r, n_sub)} for r in range(1, n_sub)]
    reached = [after, before] + peers + [patch(r) for r in (1, 2, -1, -2)]
    barrier = pltpu.get_barrier_semaphore()
    for to in reached:
        pl.semaphore_signal(barrier, inc=1, device_id=to, device_id_type=MESH)
    pool_rows = pool.shape[0]
    my_pool = pools.at[at(me, pool_rows), :]
    my_pool[...] = pool[...]

    load_nodes.wait()
    raw2 = split2(nodes_v[...])
    for k in range(2):
        fh_sent[k] = halves(dot(one_hot(column(f_halo[k : k + 1, :]), rows), raw2))
    pl.semaphore_wait(barrier, len(reached))
    fine_halo = [
        send(fh_sent.at[k], fh_got.at[k], fh_s.at[k], fh_r.at[k], to) for k, to in ((0, after), (1, before))
    ]
    pool_copies = [send(my_pool, my_pool, pl_s.at[r], pl_r.at[r], to) for r, to in enumerate(peers)]

    load_ei.wait()
    load_fs.wait()
    send_w = packed(ei_v[0, 0:W, :])
    recv_w = packed(ei_v[0, W : 2 * W, :])
    table[0:rows, :] = split2(halves(dot(raw2, send_w)))
    table[rows : rows + 2 * W, :] = packed(ei_v[0, 2 * W : 3 * W, :])

    def sender_columns(i):
        cols = []
        for k in range(degree):
            for j in range(TILE // W):
                cols.append(column(fs_v[k : k + 1, pl.ds(pl.multiple_of(i * TILE + j * W, W), W)]))
        return jnp.concatenate(cols, axis=0)

    def first_pass(i, carry):
        pltpu.make_async_copy(f_edges.at[:, pl.ds(0, TILE), :], fe_v.at[i], edge_sem.at[i]).wait()
        received = mm(nodes_v[at(i, TILE), :], recv_w)
        e2 = jnp.concatenate([split2(fe_v[i, k]) for k in range(degree)], axis=0)
        left = jnp.concatenate([one_hot(sender_columns(i), rows), e2], axis=1)
        zs[i] = halves(dot(left, table[0 : rows + 2 * W, :])) + jnp.concatenate([received] * degree, axis=0)
        return carry

    lax.fori_loop(0, tiles, first_pass, 0)
    for c in load_rest:
        c.wait()

    def level_weights(n):
        node_w = jnp.concatenate([packed(ni_v[n, 0:W, :]), packed(ni_v[n, W : 2 * W, :])], axis=0)
        return packed(centred_columns(eo_v[n])), node_w, packed(centred_columns(no_v[n]))

    out_w, node_w, last_w = level_weights(0)
    for c in fine_halo:
        c.wait_recv()
    halo_table = split2(mm(fh_got[...].reshape(2 * W, W), send_w))

    def second_pass(i, carry):
        hot = one_hot(sender_columns(i) - rows, 2 * W)
        hidden = jnp.maximum(zs[i] + halves(dot(hot, halo_table)), 0.0)
        message = scaled(mm(hidden, out_w))
        summed = fe_v[i, 0] + message[0:TILE]
        for k in range(1, degree):
            summed = summed + (fe_v[i, k] + message[k * TILE : (k + 1) * TILE])
        new = node_update(nodes_v[at(i, TILE), :], summed, node_w, last_w)
        new_v[at(i, TILE), :] = new
        news[at(i, TILE), :] = split2(new)
        return carry

    lax.fori_loop(0, tiles, second_pass, 0)

    def pair_sum(block, buf, ss, rs, r, size):
        return send(block.at[at(1 - core, size), :], buf.at[r], ss.at[r], rs.at[r], partner)

    pair = {}
    for r in (2, 1, 3, 0):
        first = pl.multiple_of(column_of(r) * 2 * share, 2 * share)
        sums_v[r] = halves(dot(one_hot_t(pool, first, 2 * share, pool_rows), news[...]))
        pair[r] = pair_sum(sums_v.at[r], pair_buf, pair_s, pair_r, r, share)
        if r == 1:
            pair[2].wait_recv()
            comb[2] = sums_v[2, at(core, share), :] + pair_buf[2]

    class RingSum:
        def __init__(self, part, stage, relay, arrive, ss, rs, half):
            self.part, self.stage, self.relay, self.arrive = part, stage, relay, arrive
            self.ss, self.rs, self.half = ss, rs, half

        def cut(self, r, h):
            return self.part.at[r, pl.ds(h * self.half, self.half), :]

        def far(self):
            self.relayed = [
                send(self.cut(2, h), self.relay.at[h], self.ss.at[h], self.rs.at[h], chip(1 - 2 * h)) for h in range(2)
            ]

        def near(self):
            self.plain = [
                send(self.cut(1 + 2 * h, 1 - h), self.arrive.at[h, 1 - h], self.ss.at[2 + h], self.rs.at[2 + h],
                     chip(1 - 2 * h))
                for h in range(2)
            ]

        def pass_on(self):
            self.joint = []
            for h in range(2):
                self.relayed[h].wait_recv()
                self.stage[h] = self.cut(1 + 2 * h, h)[...] + self.relay[h]
                self.joint.append(
                    send(self.stage.at[h], self.arrive.at[h, h], self.ss.at[4 + h], self.rs.at[4 + h], chip(1 - 2 * h))
                )

        def total(self):
            for c in self.plain + self.joint:
                c.wait_recv()
            return jnp.concatenate(
                [self.cut(0, h)[...] + self.arrive[0, h] + self.arrive[1, h] for h in range(2)], axis=0
            )

    sums = RingSum(comb, stage, relay_in, arrive, rs_s, rs_r, share // 2)
    sums.far()
    for r in (1, 3):
        pair[r].wait_recv()
        comb[r] = sums_v[r, at(core, share), :] + pair_buf[r]
    sums.near()
    pair[0].wait_recv()
    comb[0] = sums_v[0, at(core, share), :] + pair_buf[0]
    for c in load_later:
        c.wait()
    for k in range(k_q):
        row = qs_v[k : k + 1, at(me, share)]
        col = jnp.concatenate([column(row[:, j * W : (j + 1) * W]) for j in range(share // W)], axis=0)
        oh_q[k * share : (k + 1) * share, :] = one_hot(col, q_rows + 2 * W)
    sums.pass_on()
    for k in range(2):
        oh_h[k * W : (k + 1) * W, :] = one_hot(column(q_halo[k : k + 1, :]), q_rows)
    for c in pool_copies:
        c.wait_recv()
    counts = counts_of(pools, me * share, share, pools.shape[0])
    q_send_w = packed(ei_v[1, 0:W, :])
    q = sums.total() / counts
    tab[at(me, share), :] = mm(q, q_send_w)

    class RingGather:
        def __init__(self, buf, ss, rs, size):
            self.buf, self.ss, self.rs, self.size, self.half = buf, ss, rs, size, size // 2
            self.n, self.shared = 0, []
            self.from_near = {}
            for h in range(2):
                for way in range(2):
                    self.from_near[way, h ^ way] = self.go(0, h ^ way, chip(1 - 2 * way))
            for h in range(2):
                self.share_half(0, h)

        def cut(self, r, h):
            t = 2 * lax.rem(x + r + n_x, n_x) + core
            return self.buf.at[pl.ds(pl.multiple_of(t * self.size + h * self.half, self.half), self.half), :]

        def go(self, r, h, to):
            block = self.cut(r, h)
            c = send(block, block, self.ss.at[self.n], self.rs.at[self.n], to)
            self.n += 1
            return c

        def share_half(self, r, h):
            self.shared.append(self.go(r, h, partner))

        def pass_on(self):
            self.from_far = []
            for way in range(2):
                self.from_near[way, way].wait_recv()
                self.from_far.append(self.go(2 * way - 1, way, chip(1 - 2 * way)))
            for way in range(2):
                self.share_half(2 * way - 1, way)
            for way in range(2):
                self.from_near[way, 1 - way].wait_recv()
                self.share_half(2 * way - 1, 1 - way)

        def take_far(self):
            for way in range(2):
                self.from_far[way].wait_recv()
                self.share_half(2, way)

        def finish(self):
            for c in self.shared:
                c.wait_recv()

    around = RingGather(tab, ag_s, ag_r, share)
    q_recv = mm(q, packed(ei_v[1, W : 2 * W, :]))
    around.pass_on()
    edge_w = packed(ei_v[1, 2 * W : 3 * W, :])
    for k in range(k_q):
        base_v[k * share : (k + 1) * share, :] = mm(qe_v[pl.ds(k, share, stride=k_q), :], edge_w) + q_recv
    around.take_far()
    q_out_w, q_node_w, q_last_w = level_weights(1)
    own_pool = q_pool[pl.ds(me * (share // W), share // W), :]
    sub = sublanes(s_rows)
    hot16 = jnp.concatenate(
        [ones_where(jnp.broadcast_to(own_pool[j : j + 1, :], (s_rows, W)) == sub) for j in range(share // W)], axis=1
    )
    around.finish()
    table2 = split2(tab[0:q_rows, :])
    hsent[...] = halves(dot(oh_h[...], table2))
    halo = [
        send(hsent.at[pl.ds(k * W, W), :], tab.at[pl.ds(q_rows + k * W, W), :], h_s.at[k], h_r.at[k], patch(r))
        for k, r in ((0, 1), (1, -1))
    ]
    base = base_v[...] + halves(dot(oh_q[:, 0:q_rows], table2))
    for c in halo:
        c.wait_recv()
    halo2 = split2(tab[pl.ds(q_rows, 2 * W), :])
    hid = jnp.maximum(base + halves(dot(oh_q[:, q_rows : q_rows + 2 * W], halo2)), 0.0)
    msg = scaled(mm(hid, q_out_w))
    summed = None
    for k in range(k_q):
        term = qe_v[pl.ds(k, share, stride=k_q), :] + msg[k * share : (k + 1) * share]
        summed = term if summed is None else summed + term
    q_new = node_update(q, summed, q_node_w, q_last_w)
    qall[at(me, share), :] = q_new

    p16[...] = halves(dot(hot16, split2(q_new)))
    pair = {}
    for r in (2, 1, 3, 0):
        pair[r] = pair_sum(p16.at[at(column_of(r), 2 * s_share), :], pair16, pair16_s, pair16_r, r, s_share)
    sums = RingSum(comb16, stage16, relay16, arrive16, rs16_s, rs16_r, s_share // 2)
    for r in (2, 1, 3, 0):
        pair[r].wait_recv()
        t = 2 * column_of(r) + core
        comb16[r] = p16[at(t, s_share), :] + pair16[r]
        if r == 2:
            sums.far()
        if r == 3:
            sums.near()
    c_counts = counts_of(q_pool, me * s_share, s_share, q_pool.shape[0])
    c_send_w = packed(ei_v[2, 0:W, :])
    sums.pass_on()
    q_around = RingGather(qall, qg_s, qg_r, share)
    c_recv_w = packed(ei_v[2, W : 2 * W, :])
    c_edge_w = packed(ei_v[2, 2 * W : 3 * W, :])
    c = sums.total() / c_counts
    mine = pl.ds(pl.multiple_of(core * s_share, s_share), s_share)
    zt[p, mine, :] = mm(c, c_send_w)

    arrivals = {}

    def relay(src, sign, dist, last):
        block = zt.at[src, mine, :]
        way = 0 if sign > 0 else 1
        for hop in (2, 1):
            if dist + hop <= last:
                arrivals[sign, dist + hop] = send(
                    block, block, z_s.at[way, dist + hop], z_r.at[way, dist + hop], patch(sign * hop)
                )

    shared = []

    def hand_over(src, slot):
        block = zt.at[src, mine, :]
        shared.append(send(block, block, d_s.at[slot], d_r.at[slot], partner))

    far, near = n_patch // 2, n_patch - n_patch // 2 - 1
    limits = {1: far, -1: near}
    for sign in (1, -1):
        relay(p, sign, 0, limits[sign])
    hand_over(p, 0)

    def hot_pool():
        for j in range(rows // W):
            oh_p[j * W : (j + 1) * W, :] = one_hot(column(pool[j : j + 1, :]), q_rows)

    def hot_senders():
        for n, r in enumerate((2, 1, 3, 0)):
            for k in range(k_s):
                g = column(cs_v[k : k + 1, at(column_of(r), W)])
                g = jnp.where(core == 0, g[0:s_share], g[s_share : 2 * s_share])
                g = jnp.where((g // W) % n_x == x, (g // s_rows) * W + g % W, -1)
                first = n * k_s * s_share + k * s_share
                oh_c[first : first + s_share, :] = one_hot(g, n_patch * W)

    def hot_last():
        of_quarter = jnp.concatenate(
            [column(q_pool[j : j + 1, :]).astype(F32) for j in range(q_rows // W)], axis=0
        )
        target = halves(dot(oh_p[...], split2(of_quarter))).astype(jnp.int32)
        oh_t[...] = one_hot(target, s_rows)

    c_recv = mm(c, c_recv_w)
    c_base = []
    for k in range(k_s):
        c_base.append(mm(ce_v[pl.ds(k, s_share, stride=k_s), :], c_edge_w) + c_recv)

    def add_quarter():
        q_around.finish()
        new_v[...] = new_v[...] + halves(dot(oh_p[...], split2(qall[...])))

    between = {2: [q_around.pass_on, hot_senders], 4: [q_around.take_far, hot_pool], 6: [hot_last], 8: []}
    for dist in range(2, far + 2, 2):
        for work in between.get(dist, []):
            work()
        for d in (dist, dist - 1):
            for sign in (1, -1):
                if d <= limits[sign]:
                    arrivals[sign, d].wait_recv()
                    src = lax.rem(p - sign * d + n_patch, n_patch)
                    if d == dist:
                        relay(src, sign, d, limits[sign])
                    hand_over(src, d if sign > 0 else far + d)
    c_out_w, c_node_w, c_last_w = level_weights(2)
    for s in shared:
        s.wait_recv()
    ztable = split2(zt[...].reshape(n_patch * 2 * s_share, W))
    size = k_s * s_share
    sums = RingSum(gpart, gstage, grelay, garrive, g_s, g_r, size // 2)
    for n, r in enumerate((2, 1, 3, 0)):
        gpart[r] = halves(dot(oh_c[n * size : (n + 1) * size, :], ztable))
        if r == 2:
            sums.far()
        if r == 3:
            sums.near()
    sums.pass_on()
    add_quarter()
    hid = jnp.maximum(jnp.concatenate(c_base, axis=0) + sums.total(), 0.0)
    msg = scaled(mm(hid, c_out_w))
    summed = None
    for k in range(k_s):
        term = ce_v[pl.ds(k, s_share, stride=k_s), :] + msg[k * s_share : (k + 1) * s_share]
        summed = term if summed is None else summed + term
    ctab[at(me, s_share), :] = node_update(c, summed, c_node_w, c_last_w)
    c_around = RingGather(ctab, cg_s, cg_r, s_share)
    c_around.pass_on()
    c_around.take_far()
    c_around.finish()
    out[...] = new_v[...] + halves(dot(oh_t[...], split2(ctab[...])))
    for s in send.all:
        s.wait_send()


def all_levels(n_patch, n_sub, nodes, f_edges, f_senders, f_halo, pool, q_edges, q_senders, q_halo, q_pool, c_edges,
               c_senders, edge_in, edge_out, node_in, node_out):
    any_ = pl.BlockSpec(memory_space=pl.ANY)
    vm = pl.BlockSpec(memory_space=pltpu.VMEM)
    degree, rows, _ = f_edges.shape
    k_q, q_rows = q_senders.shape
    share = q_rows // n_sub
    k_s = c_senders.shape[0]
    s_rows = c_senders.shape[1] // n_patch
    s_share = s_rows // n_sub
    n_x = n_sub // 2
    dma = pltpu.SemaphoreType.DMA
    v = lambda *shape: pltpu.VMEM(shape, F32)
    b = lambda *shape: pltpu.VMEM(shape, BF)
    i32 = lambda *shape: pltpu.VMEM(shape, jnp.int32)
    gsems = [dma((14,)), dma((14,))]
    return pl.pallas_call(
        functools.partial(levels_kernel, n_patch, n_sub),
        name="all_levels",
        out_shape=jax.ShapeDtypeStruct((rows, W), F32),
        in_specs=[any_, any_, any_, vm, vm, any_, any_, vm, vm, any_, any_, any_, any_, any_, any_],
        out_specs=vm,
        scratch_shapes=[
            v(rows, W), v(rows // TILE, degree, TILE, W), i32(degree, rows),
            v(share * k_q, W), i32(k_q, q_rows), v(s_share * k_s, W), i32(k_s, s_rows),
            v(*edge_in.shape), v(*edge_out.shape), v(*node_in.shape), v(*node_out.shape),
            i32(n_sub * pool.shape[0], W), v(2, W, W), v(2, W, W),
            b(rows + 2 * W, 2 * W), b(rows, 2 * W), v(rows // TILE, degree * TILE, W), v(rows, W),
            v(n_x, 2 * share, W), v(n_x, share, W), v(n_x, share, W),
            v(2, share // 2, W), v(2, share // 2, W), v(2, 2, share // 2, W),
            v(q_rows + 2 * W, W), v(2 * W, W), v(q_rows, W),
            b(k_q * share, q_rows + 2 * W), b(2 * W, q_rows), b(n_x * k_s * s_share, n_patch * W),
            b(rows, q_rows), b(rows, s_rows), v(k_q * share, W),
            v(s_rows, W), v(n_x, s_share, W), v(n_x, s_share, W),
            v(2, s_share // 2, W), v(2, s_share // 2, W), v(2, 2, s_share // 2, W),
            v(n_patch, 2 * s_share, W), v(n_x, k_s * s_share, W),
            v(2, k_s * s_share // 2, W), v(2, k_s * s_share // 2, W), v(2, 2, k_s * s_share // 2, W), v(s_rows, W),
            dma((10,)), dma((rows // TILE,)), dma((2,)), dma((2,)), dma((n_sub - 1,)), dma((n_sub - 1,)),
            dma((n_x,)), dma((n_x,)), dma((6,)), dma((6,)), *gsems, dma((2,)), dma((2,)),
            dma((n_x,)), dma((n_x,)), dma((6,)), dma((6,)), *gsems,
            dma((2, n_patch)), dma((2, n_patch)), dma((n_patch,)), dma((n_patch,)),
            dma((6,)), dma((6,)), *gsems,
        ],
        compiler_params=pltpu.CompilerParams(collective_id=0, has_side_effects=True, vmem_limit_bytes=VMEM_LIMIT),
    )(nodes, f_edges, f_senders, f_halo, pool, q_edges, q_senders, q_halo, q_pool, c_edges, c_senders, edge_in,
      edge_out, node_in, node_out)


def on_device(n_patch, n_sub, fine_nodes, fine_edges, fine_senders, fine_halo, fine_pool, quarter_edges,
              quarter_senders, quarter_halo, quarter_pool, coarse_edges, coarse_senders, edge_in, edge_out, node_in,
              node_out):
    return all_levels(n_patch, n_sub, fine_nodes, fine_edges.transpose(1, 0, 2), fine_senders.T, fine_halo,
                      fine_pool.reshape(-1, W), quarter_edges.reshape(-1, W), quarter_senders.T, quarter_halo,
                      quarter_pool.reshape(-1, W), coarse_edges.reshape(-1, W), coarse_senders.T, edge_in, edge_out,
                      node_in, node_out)


def solution(mesh):
    both = ("groups", "patch", "sub")
    halfway = ("groups", "patch")
    in_specs = (
        P(both, None),
        P(both, None, None),
        P(both, None),
        P(both, None),
        P(both),
        P(halfway, None, None),
        P(halfway, None),
        P(halfway, None),
        P(halfway),
        P(both, None, None),
        P("groups", None),
        P(),
        P(),
        P(),
        P(),
    )
    return jax.shard_map(
        functools.partial(on_device, mesh.shape["patch"], mesh.shape["sub"]),
        mesh=mesh,
        in_specs=in_specs,
        out_specs=P(both, None),
        check_vma=False,
    )
```

profile of v0, /device:TPU:33, one launch (start us, length us, event | category | flops | bytes accessed | tf_op | source)
XLA Modules:
  0.0 107.2 jit_solution(5082999742924404595)
XLA Ops:
  0.0 105.3 %all_levels.1 = f32[1024,128]{1,0:T(8,128)} custom-call(f32[1024,128]{1,0:T(8,128)} %nodes.1, f32[6,1024,128]{2,1,0:T(8,128)} %bitcast.9, s32[6,1024]{1,0:T(8,128)} %bitcast.12, s32[2,128]{1,0:T(2,128)} %f_halo.1, s32[8,128]{1,0:T(8,128)} %bitcast.15, f32[8192,128]{1,0:T(8,128)} %bitcast.8, s32[4,2048]{1,0:T(4,128)} %bitcast.13, s32[2,128]{1,0:T(2,128)} %q_halo.1, ...), custom_call_target="tpu_custom_call" | custom-call | tf_op jit(solution)/shard_map/all_levels/pallas_call | solution.py:523
  105.3 1.9 %copy.17 = f32[1024,128]{1,0:T(8,128)} copy(f32[1024,128]{1,0:T(8,128)} %all_levels.1) | data formatting | bytes 1048576
where the time goes:
time: 108 us; the launch traced here: 107 us
  Pallas kernels  105 us (97%)
  local copies, waits for them, and re-layouts  1.87 us (2%)
    pallas_call x1, Pallas kernels, all_levels(): pl.pallas_call(functools.partial(levels_kernel, n_patch, n_sub), name='al...  105 us

commit v1 on v0

--- a/solution.py
+++ b/solution.py
@@ -85,7 +85,7 @@
     return jnp.sum(acc, axis=1, keepdims=True)
 
 
-TILE = 256
+TILE = 512
 
 
 class Sends:
@@ -238,18 +238,6 @@
 
     lax.fori_loop(0, tiles, second_pass, 0)
 
-    def pair_sum(block, buf, ss, rs, r, size):
-        return send(block.at[at(1 - core, size), :], buf.at[r], ss.at[r], rs.at[r], partner)
-
-    pair = {}
-    for r in (2, 1, 3, 0):
-        first = pl.multiple_of(column_of(r) * 2 * share, 2 * share)
-        sums_v[r] = halves(dot(one_hot_t(pool, first, 2 * share, pool_rows), news[...]))
-        pair[r] = pair_sum(sums_v.at[r], pair_buf, pair_s, pair_r, r, share)
-        if r == 1:
-            pair[2].wait_recv()
-            comb[2] = sums_v[2, at(core, share), :] + pair_buf[2]
-
     class RingSum:
         def __init__(self, part, stage, relay, arrive, ss, rs, half):
             self.part, self.stage, self.relay, self.arrive = part, stage, relay, arrive
@@ -286,8 +274,40 @@
                 [self.cut(0, h)[...] + self.arrive[0, h] + self.arrive[1, h] for h in range(2)], axis=0
             )
 
+    def hot_pool():
+        for j in range(rows // W):
+            oh_p[j * W : (j + 1) * W, :] = one_hot(column(pool[j : j + 1, :]), q_rows)
+
+    def hot_senders():
+        for n, r in enumerate((2, 1, 3, 0)):
+            for k in range(k_s):
+                g = column(cs_v[k : k + 1, at(column_of(r), W)])
+                g = jnp.where(core == 0, g[0:s_share], g[s_share : 2 * s_share])
+                g = jnp.where((g // W) % n_x == x, (g // s_rows) * W + g % W, -1)
+                first = n * k_s * s_share + k * s_share
+                oh_c[first : first + s_share, :] = one_hot(g, n_patch * W)
+
+    def hot_last():
+        of_quarter = jnp.concatenate(
+            [column(q_pool[j : j + 1, :]).astype(F32) for j in range(q_rows // W)], axis=0
+        )
+        target = halves(dot(oh_p[...], split2(of_quarter))).astype(jnp.int32)
+        oh_t[...] = one_hot(target, s_rows)
+
+    def pair_sum(block, buf, ss, rs, r, size):
+        return send(block.at[at(1 - core, size), :], buf.at[r], ss.at[r], rs.at[r], partner)
+
+    pair = {}
     sums = RingSum(comb, stage, relay_in, arrive, rs_s, rs_r, share // 2)
-    sums.far()
+    for r in (2, 1, 3, 0):
+        first = pl.multiple_of(column_of(r) * 2 * share, 2 * share)
+        sums_v[r] = halves(dot(one_hot_t(pool, first, 2 * share, pool_rows), news[...]))
+        pair[r] = pair_sum(sums_v.at[r], pair_buf, pair_s, pair_r, r, share)
+        if r == 1:
+            pair[2].wait_recv()
+            comb[2] = sums_v[2, at(core, share), :] + pair_buf[2]
+            sums.far()
+
     for r in (1, 3):
         pair[r].wait_recv()
         comb[r] = sums_v[r, at(core, share), :] + pair_buf[r]
@@ -306,6 +326,7 @@
     for c in pool_copies:
         c.wait_recv()
     counts = counts_of(pools, me * share, share, pools.shape[0])
+    hot_pool()
     q_send_w = packed(ei_v[1, 0:W, :])
     q = sums.total() / counts
     tab[at(me, share), :] = mm(q, q_send_w)
@@ -356,6 +377,7 @@
 
     around = RingGather(tab, ag_s, ag_r, share)
     q_recv = mm(q, packed(ei_v[1, W : 2 * W, :]))
+    hot_senders()
     around.pass_on()
     edge_w = packed(ei_v[1, 2 * W : 3 * W, :])
     for k in range(k_q):
@@ -375,6 +397,7 @@
         for k, r in ((0, 1), (1, -1))
     ]
     base = base_v[...] + halves(dot(oh_q[:, 0:q_rows], table2))
+    hot_last()
     for c in halo:
         c.wait_recv()
     halo2 = split2(tab[pl.ds(q_rows, 2 * W), :])
@@ -433,26 +456,6 @@
         relay(p, sign, 0, limits[sign])
     hand_over(p, 0)
 
-    def hot_pool():
-        for j in range(rows // W):
-            oh_p[j * W : (j + 1) * W, :] = one_hot(column(pool[j : j + 1, :]), q_rows)
-
-    def hot_senders():
-        for n, r in enumerate((2, 1, 3, 0)):
-            for k in range(k_s):
-                g = column(cs_v[k : k + 1, at(column_of(r), W)])
-                g = jnp.where(core == 0, g[0:s_share], g[s_share : 2 * s_share])
-                g = jnp.where((g // W) % n_x == x, (g // s_rows) * W + g % W, -1)
-                first = n * k_s * s_share + k * s_share
-                oh_c[first : first + s_share, :] = one_hot(g, n_patch * W)
-
-    def hot_last():
-        of_quarter = jnp.concatenate(
-            [column(q_pool[j : j + 1, :]).astype(F32) for j in range(q_rows // W)], axis=0
-        )
-        target = halves(dot(oh_p[...], split2(of_quarter))).astype(jnp.int32)
-        oh_t[...] = one_hot(target, s_rows)
-
     c_recv = mm(c, c_recv_w)
     c_base = []
     for k in range(k_s):
@@ -462,10 +465,8 @@
         q_around.finish()
         new_v[...] = new_v[...] + halves(dot(oh_p[...], split2(qall[...])))
 
-    between = {2: [q_around.pass_on, hot_senders], 4: [q_around.take_far, hot_pool], 6: [hot_last], 8: []}
+    between = {2: q_around.pass_on, 4: q_around.take_far}
     for dist in range(2, far + 2, 2):
-        for work in between.get(dist, []):
-            work()
         for d in (dist, dist - 1):
             for sign in (1, -1):
                 if d <= limits[sign]:
@@ -474,6 +475,8 @@
                     if d == dist:
                         relay(src, sign, d, limits[sign])
                     hand_over(src, d if sign > 0 else far + d)
+        if dist in between:
+            between[dist]()
     c_out_w, c_node_w, c_last_w = level_weights(2)
     for s in shared:
         s.wait_recv()

time: 108 us -> 104 us (0.963)
  Pallas kernels: 105 us -> 101 us
    pallas_call x1, Pallas kernels: 105 us -> 101 us  [all_levels(): pl.pallas_call(functools.partial(levels_kernel, n_patch, n_sub), name='al...]
where the time goes in v1:
time: 104 us; the launch traced here: 103 us
  Pallas kernels  101 us (97%)
  local copies, waits for them, and re-layouts  1.87 us (2%)
    pallas_call x1, Pallas kernels, all_levels(): pl.pallas_call(functools.partial(levels_kernel, n_patch, n_sub), name='al...  101 us

profile of v1, /device:TPU:33, one launch (start us, length us, event | category | flops | bytes accessed | tf_op | source)
XLA Modules:
  0.0 103.3 jit_solution(7129669127584501074)
XLA Ops:
  0.0 101.4 %all_levels.1 = f32[1024,128]{1,0:T(8,128)} custom-call(f32[1024,128]{1,0:T(8,128)} %nodes.1, f32[6,1024,128]{2,1,0:T(8,128)} %bitcast.9, s32[6,1024]{1,0:T(8,128)} %bitcast.12, s32[2,128]{1,0:T(2,128)} %f_halo.1, s32[8,128]{1,0:T(8,128)} %bitcast.15, f32[8192,128]{1,0:T(8,128)} %bitcast.8, s32[4,2048]{1,0:T(4,128)} %bitcast.13, s32[2,128]{1,0:T(2,128)} %q_halo.1, ...), custom_call_target="tpu_custom_call" | custom-call | tf_op jit(solution)/shard_map/all_levels/pallas_call | solution.py:526
  101.4 1.9 %copy.17 = f32[1024,128]{1,0:T(8,128)} copy(f32[1024,128]{1,0:T(8,128)} %all_levels.1) | data formatting | bytes 1048576

commit v2 on v1

--- a/solution.py
+++ b/solution.py
@@ -116,7 +116,7 @@
                   p16, pair16, comb16, stage16, relay16, arrive16, zt, gpart, gstage, grelay, garrive, ctab,
                   load_sem, edge_sem, fh_s, fh_r, pl_s, pl_r,
                   pair_s, pair_r, rs_s, rs_r, ag_s, ag_r, h_s, h_r,
-                  pair16_s, pair16_r, rs16_s, rs16_r, qg_s, qg_r, z_s, z_r, d_s, d_r, g_s, g_r, cg_s, cg_r):
+                  pair16_s, pair16_r, rs16_s, rs16_r, qg_s, qg_r, z_s, z_r, d_s, d_r, g_s, g_r, cg_s, cg_r, store_sem):
     p, me = lax.axis_index("patch"), lax.axis_index("sub")
     core = lax.rem(me, 2)
     x = me // 2
@@ -239,33 +239,47 @@
     lax.fori_loop(0, tiles, second_pass, 0)
 
     class RingSum:
-        def __init__(self, part, stage, relay, arrive, ss, rs, half):
+        def __init__(self, part, stage, relay, arrive, ss, rs, half, pieces):
             self.part, self.stage, self.relay, self.arrive = part, stage, relay, arrive
-            self.ss, self.rs, self.half = ss, rs, half
+            self.ss, self.rs, self.half, self.pieces = ss, rs, half, pieces
+            self.size = half // pieces
 
         def cut(self, r, h):
             return self.part.at[r, pl.ds(h * self.half, self.half), :]
 
+        def piece(self, i):
+            return pl.ds(i * self.size, self.size)
+
+        def part_piece(self, r, h, i):
+            return self.part.at[r, pl.ds(h * self.half + i * self.size, self.size), :]
+
         def far(self):
-            self.relayed = [
-                send(self.cut(2, h), self.relay.at[h], self.ss.at[h], self.rs.at[h], chip(1 - 2 * h)) for h in range(2)
-            ]
+            self.relayed = {}
+            for i in range(self.pieces):
+                for h in range(2):
+                    k = h * self.pieces + i
+                    self.relayed[h, i] = send(self.part_piece(2, h, i), self.relay.at[h, self.piece(i), :],
+                                              self.ss.at[k], self.rs.at[k], chip(1 - 2 * h))
 
         def near(self):
-            self.plain = [
-                send(self.cut(1 + 2 * h, 1 - h), self.arrive.at[h, 1 - h], self.ss.at[2 + h], self.rs.at[2 + h],
-                     chip(1 - 2 * h))
-                for h in range(2)
-            ]
+            self.plain = []
+            for h in range(2):
+                k = 2 * self.pieces + h
+                self.plain.append(send(self.cut(1 + 2 * h, 1 - h), self.arrive.at[h, 1 - h], self.ss.at[k],
+                                       self.rs.at[k], chip(1 - 2 * h)))
 
         def pass_on(self):
             self.joint = []
-            for h in range(2):
-                self.relayed[h].wait_recv()
-                self.stage[h] = self.cut(1 + 2 * h, h)[...] + self.relay[h]
-                self.joint.append(
-                    send(self.stage.at[h], self.arrive.at[h, h], self.ss.at[4 + h], self.rs.at[4 + h], chip(1 - 2 * h))
-                )
+            for i in range(self.pieces):
+                for h in range(2):
+                    self.relayed[h, i].wait_recv()
+                    at_piece = self.piece(i)
+                    self.stage[h, at_piece, :] = (
+                        self.part_piece(1 + 2 * h, h, i)[...] + self.relay[h, at_piece, :]
+                    )
+                    k = 2 * self.pieces + 2 + h * self.pieces + i
+                    self.joint.append(send(self.stage.at[h, at_piece, :], self.arrive.at[h, h, at_piece, :],
+                                           self.ss.at[k], self.rs.at[k], chip(1 - 2 * h)))
 
         def total(self):
             for c in self.plain + self.joint:
@@ -298,7 +312,7 @@
         return send(block.at[at(1 - core, size), :], buf.at[r], ss.at[r], rs.at[r], partner)
 
     pair = {}
-    sums = RingSum(comb, stage, relay_in, arrive, rs_s, rs_r, share // 2)
+    sums = RingSum(comb, stage, relay_in, arrive, rs_s, rs_r, share // 2, 2)
     for r in (2, 1, 3, 0):
         first = pl.multiple_of(column_of(r) * 2 * share, 2 * share)
         sums_v[r] = halves(dot(one_hot_t(pool, first, 2 * share, pool_rows), news[...]))
@@ -332,50 +346,54 @@
     tab[at(me, share), :] = mm(q, q_send_w)
 
     class RingGather:
-        def __init__(self, buf, ss, rs, size):
+        def __init__(self, buf, ss, rs, size, pieces):
             self.buf, self.ss, self.rs, self.size, self.half = buf, ss, rs, size, size // 2
+            self.pieces = pieces
             self.n, self.shared = 0, []
-            self.from_near = {}
-            for h in range(2):
+            self.first, self.second = {}, {}
+            for i in range(pieces):
                 for way in range(2):
-                    self.from_near[way, h ^ way] = self.go(0, h ^ way, chip(1 - 2 * way))
+                    self.first[way, i] = self.go(0, way, chip(1 - 2 * way), i)
+            for way in range(2):
+                self.second[way] = self.go(0, 1 - way, chip(1 - 2 * way))
             for h in range(2):
                 self.share_half(0, h)
 
-        def cut(self, r, h):
+        def go(self, r, h, to, i=None):
             t = 2 * lax.rem(x + r + n_x, n_x) + core
-            return self.buf.at[pl.ds(pl.multiple_of(t * self.size + h * self.half, self.half), self.half), :]
-
-        def go(self, r, h, to):
-            block = self.cut(r, h)
+            rows_ = self.half if i is None else self.half // self.pieces
+            first = t * self.size + h * self.half + (0 if i is None else i * rows_)
+            block = self.buf.at[pl.ds(pl.multiple_of(first, rows_), rows_), :]
             c = send(block, block, self.ss.at[self.n], self.rs.at[self.n], to)
             self.n += 1
             return c
 
-        def share_half(self, r, h):
-            self.shared.append(self.go(r, h, partner))
+        def share_half(self, r, h, i=None):
+            self.shared.append(self.go(r, h, partner, i))
 
         def pass_on(self):
-            self.from_far = []
-            for way in range(2):
-                self.from_near[way, way].wait_recv()
-                self.from_far.append(self.go(2 * way - 1, way, chip(1 - 2 * way)))
+            self.from_far = {}
+            for i in range(self.pieces):
+                for way in range(2):
+                    self.first[way, i].wait_recv()
+                    self.from_far[way, i] = self.go(2 * way - 1, way, chip(1 - 2 * way), i)
             for way in range(2):
                 self.share_half(2 * way - 1, way)
             for way in range(2):
-                self.from_near[way, 1 - way].wait_recv()
+                self.second[way].wait_recv()
                 self.share_half(2 * way - 1, 1 - way)
 
         def take_far(self):
-            for way in range(2):
-                self.from_far[way].wait_recv()
-                self.share_half(2, way)
+            for i in range(self.pieces):
+                for way in range(2):
+                    self.from_far[way, i].wait_recv()
+                    self.share_half(2, way, i)
 
         def finish(self):
             for c in self.shared:
                 c.wait_recv()
 
-    around = RingGather(tab, ag_s, ag_r, share)
+    around = RingGather(tab, ag_s, ag_r, share, 2)
     q_recv = mm(q, packed(ei_v[1, W : 2 * W, :]))
     hot_senders()
     around.pass_on()
@@ -414,7 +432,7 @@
     pair = {}
     for r in (2, 1, 3, 0):
         pair[r] = pair_sum(p16.at[at(column_of(r), 2 * s_share), :], pair16, pair16_s, pair16_r, r, s_share)
-    sums = RingSum(comb16, stage16, relay16, arrive16, rs16_s, rs16_r, s_share // 2)
+    sums = RingSum(comb16, stage16, relay16, arrive16, rs16_s, rs16_r, s_share // 2, 1)
     for r in (2, 1, 3, 0):
         pair[r].wait_recv()
         t = 2 * column_of(r) + core
@@ -426,7 +444,7 @@
     c_counts = counts_of(q_pool, me * s_share, s_share, q_pool.shape[0])
     c_send_w = packed(ei_v[2, 0:W, :])
     sums.pass_on()
-    q_around = RingGather(qall, qg_s, qg_r, share)
+    q_around = RingGather(qall, qg_s, qg_r, share, 1)
     c_recv_w = packed(ei_v[2, W : 2 * W, :])
     c_edge_w = packed(ei_v[2, 2 * W : 3 * W, :])
     c = sums.total() / c_counts
@@ -482,7 +500,7 @@
         s.wait_recv()
     ztable = split2(zt[...].reshape(n_patch * 2 * s_share, W))
     size = k_s * s_share
-    sums = RingSum(gpart, gstage, grelay, garrive, g_s, g_r, size // 2)
+    sums = RingSum(gpart, gstage, grelay, garrive, g_s, g_r, size // 2, 2)
     for n, r in enumerate((2, 1, 3, 0)):
         gpart[r] = halves(dot(oh_c[n * size : (n + 1) * size, :], ztable))
         if r == 2:
@@ -498,11 +516,18 @@
         term = ce_v[pl.ds(k, s_share, stride=k_s), :] + msg[k * s_share : (k + 1) * s_share]
         summed = term if summed is None else summed + term
     ctab[at(me, s_share), :] = node_update(c, summed, c_node_w, c_last_w)
-    c_around = RingGather(ctab, cg_s, cg_r, s_share)
+    c_around = RingGather(ctab, cg_s, cg_r, s_share, 1)
     c_around.pass_on()
     c_around.take_far()
     c_around.finish()
-    out[...] = new_v[...] + halves(dot(oh_t[...], split2(ctab[...])))
+    ctable = split2(ctab[...])
+    stores = []
+    for j in range(4):
+        block = pl.ds(j * (rows // 4), rows // 4)
+        new_v[block, :] = new_v[block, :] + halves(dot(oh_t[block, :], ctable))
+        stores.append(load(new_v.at[block, :], out.at[block, :], store_sem.at[j]))
+    for c in stores:
+        c.wait()
     for s in send.all:
         s.wait_send()
 
@@ -522,13 +547,13 @@
     v = lambda *shape: pltpu.VMEM(shape, F32)
     b = lambda *shape: pltpu.VMEM(shape, BF)
     i32 = lambda *shape: pltpu.VMEM(shape, jnp.int32)
-    gsems = [dma((14,)), dma((14,))]
+    gsems = [dma((20,)), dma((20,))]
     return pl.pallas_call(
         functools.partial(levels_kernel, n_patch, n_sub),
         name="all_levels",
         out_shape=jax.ShapeDtypeStruct((rows, W), F32),
         in_specs=[any_, any_, any_, vm, vm, any_, any_, vm, vm, any_, any_, any_, any_, any_, any_],
-        out_specs=vm,
+        out_specs=any_,
         scratch_shapes=[
             v(rows, W), v(rows // TILE, degree, TILE, W), i32(degree, rows),
             v(share * k_q, W), i32(k_q, q_rows), v(s_share * k_s, W), i32(k_s, s_rows),
@@ -545,10 +570,10 @@
             v(n_patch, 2 * s_share, W), v(n_x, k_s * s_share, W),
             v(2, k_s * s_share // 2, W), v(2, k_s * s_share // 2, W), v(2, 2, k_s * s_share // 2, W), v(s_rows, W),
             dma((10,)), dma((rows // TILE,)), dma((2,)), dma((2,)), dma((n_sub - 1,)), dma((n_sub - 1,)),
-            dma((n_x,)), dma((n_x,)), dma((6,)), dma((6,)), *gsems, dma((2,)), dma((2,)),
-            dma((n_x,)), dma((n_x,)), dma((6,)), dma((6,)), *gsems,
+            dma((n_x,)), dma((n_x,)), dma((10,)), dma((10,)), *gsems, dma((2,)), dma((2,)),
+            dma((n_x,)), dma((n_x,)), dma((10,)), dma((10,)), *gsems,
             dma((2, n_patch)), dma((2, n_patch)), dma((n_patch,)), dma((n_patch,)),
-            dma((6,)), dma((6,)), *gsems,
+            dma((10,)), dma((10,)), *gsems, dma((4,)),
         ],
         compiler_params=pltpu.CompilerParams(collective_id=0, has_side_effects=True, vmem_limit_bytes=VMEM_LIMIT),
     )(nodes, f_edges, f_senders, f_halo, pool, q_edges, q_senders, q_halo, q_pool, c_edges, c_senders, edge_in,

time: 104 us -> 103 us (level)
  no operation moved by 1% of the time
where the time goes in v2:
time: 103 us
  Pallas kernels  101 us (98%)
  local copies, waits for them, and re-layouts  1.87 us (2%)
    pallas_call x1, Pallas kernels, all_levels(): pl.pallas_call(functools.partial(levels_kernel, n_patch, n_sub), name='al...  101 us

profile of v2, /device:TPU:33, one launch (start us, length us, event | category | flops | bytes accessed | tf_op | source)
XLA Modules:
  0.0 103.0 jit_solution(13140375964661446250)
XLA Ops:
  0.0 101.1 %all_levels.1 = f32[1024,128]{1,0:T(8,128)} custom-call(f32[1024,128]{1,0:T(8,128)} %nodes.1, f32[6,1024,128]{2,1,0:T(8,128)} %bitcast.9, s32[6,1024]{1,0:T(8,128)} %bitcast.12, s32[2,128]{1,0:T(2,128)} %f_halo.1, s32[8,128]{1,0:T(8,128)} %bitcast.15, f32[8192,128]{1,0:T(8,128)} %bitcast.8, s32[4,2048]{1,0:T(4,128)} %bitcast.13, s32[2,128]{1,0:T(2,128)} %q_halo.1, ...), custom_call_target="tpu_custom_call" | custom-call | tf_op jit(solution)/shard_map/all_levels/pallas_call | solution.py:551
  101.1 1.9 %copy.17 = f32[1024,128]{1,0:T(8,128)} copy(f32[1024,128]{1,0:T(8,128)} %all_levels.1) | data formatting | bytes 1048576

commit v3 on v2

--- a/solution.py
+++ b/solution.py
@@ -160,13 +160,6 @@
         load(node_in, ni_v, load_sem.at[4]),
         load(node_out, no_v, load_sem.at[5]),
     ]
-    load_later = [
-        load(q_edges.at[at(me, share * k_q), :], qe_v, load_sem.at[6]),
-        load(q_senders, qs_v, load_sem.at[7]),
-        load(c_edges, ce_v, load_sem.at[8]),
-        load(c_senders.at[:, at(p, s_rows)], cs_v, load_sem.at[9]),
-    ]
-
     after = {"patch": lax.rem(p + (me + 1) // n_sub, n_patch), "sub": lax.rem(me + 1, n_sub)}
     wrap = (n_sub - me) // n_sub
     before = {"patch": lax.rem(p + n_patch - wrap, n_patch), "sub": lax.rem(me + n_sub - 1, n_sub)}
@@ -188,6 +181,13 @@
         send(fh_sent.at[k], fh_got.at[k], fh_s.at[k], fh_r.at[k], to) for k, to in ((0, after), (1, before))
     ]
     pool_copies = [send(my_pool, my_pool, pl_s.at[r], pl_r.at[r], to) for r, to in enumerate(peers)]
+
+    load_later = [
+        load(q_edges.at[at(me, share * k_q), :], qe_v, load_sem.at[6]),
+        load(q_senders, qs_v, load_sem.at[7]),
+        load(c_edges, ce_v, load_sem.at[8]),
+        load(c_senders.at[:, at(p, s_rows)], cs_v, load_sem.at[9]),
+    ]
 
     load_ei.wait()
     load_fs.wait()

time: 103 us -> 103 us (level)
  no operation moved by 1% of the time
where the time goes in v3:
time: 103 us
  Pallas kernels  101 us (98%)
  local copies, waits for them, and re-layouts  1.87 us (2%)
    pallas_call x1, Pallas kernels, all_levels(): pl.pallas_call(functools.partial(levels_kernel, n_patch, n_sub), name='al...  101 us

profile of v3, /device:TPU:33, one launch (start us, length us, event | category | flops | bytes accessed | tf_op | source)
XLA Modules:
  0.0 103.0 jit_solution(6375417660733372819)
XLA Ops:
  0.0 101.1 %all_levels.1 = f32[1024,128]{1,0:T(8,128)} custom-call(f32[1024,128]{1,0:T(8,128)} %nodes.1, f32[6,1024,128]{2,1,0:T(8,128)} %bitcast.9, s32[6,1024]{1,0:T(8,128)} %bitcast.12, s32[2,128]{1,0:T(2,128)} %f_halo.1, s32[8,128]{1,0:T(8,128)} %bitcast.15, f32[8192,128]{1,0:T(8,128)} %bitcast.8, s32[4,2048]{1,0:T(4,128)} %bitcast.13, s32[2,128]{1,0:T(2,128)} %q_halo.1, ...), custom_call_target="tpu_custom_call" | custom-call | tf_op jit(solution)/shard_map/all_levels/pallas_call | solution.py:551
  101.1 1.9 %copy.17 = f32[1024,128]{1,0:T(8,128)} copy(f32[1024,128]{1,0:T(8,128)} %all_levels.1) | data formatting | bytes 1048576
